TPU v7x, 32 devices: a whole 2x2x4 slice. The times are simulated.
32 devices in a mesh: expert: 16 (over z, y, x), replica: 2 (over core).
Axes of the slice: x: 2, y: 2, z: 4, core: 2. Of those that a mesh axis runs over, the one named last changes fastest.
Arguments:
- tokens: bfloat16 [16384, 1024], P(('expert', 'replica')), may hold values from -6 to 6
- expert_id: int32 [16384, 1], P(('expert', 'replica')), may hold values from 0 to 15; in each aligned block of 512 rows (0 to 511, 512 to 1023, ...) at most 64 rows name the same one
- router_prob: float32 [16384], P(('expert', 'replica')), may hold values from 0.1 to 1
- keep_mask: int32 [16, 32, 2048], P('expert'), may hold values 0 or 1
- w_in: bfloat16 [16, 1024, 2048], P('expert'), may hold values from -0.1875 to 0.1875
- w_out: bfloat16 [16, 2048, 1024], P('expert'), may hold values from -0.125 to 0.125
- cotangent: bfloat16 [16384, 1024], P(('expert', 'replica')), may hold values from -0.59765625 to 0.59765625
Outputs:
- mixed: bfloat16 [16384, 1024], P(('expert', 'replica'))
- grad_in: float32 [16, 1024, 2048], P('expert', 'replica')
- grad_out: float32 [16, 2048, 1024], P('expert', 'replica')
Inputs may be any that keep to these rules, and one draw needn't show every extreme that they name: `expert_id`: among the 512 tokens of one device no expert is chosen more than 64 times; on some devices one expert is chosen exactly 64 times.
All inputs are finite; a program needn't handle non-finite values. No bound on the sum of `keep_mask` on one device may be relied on, other than what follows from the above.
Results may differ from a plain program's by a relative error of at most 0.0057.
Values may be sent and summed in bfloat16 or wider, within the bound.
A program may use at most 128 MiB of HBM per device.

v0:
```python
import functools

import jax
import jax.numpy as jnp
from jax import lax
from jax.experimental import pallas as pl
from jax.experimental.pallas import tpu as pltpu
from jax.sharding import PartitionSpec as P

KEEP_SCALE = 4.0 / 3.0
MESH = pl.DeviceIdType.MESH


def gelu_parts(pre):
    inner = 0.7978845608 * (pre + 0.044715 * pre * pre * pre)
    tanh_v = jnp.tanh(inner)
    value = 0.5 * pre * (1.0 + tanh_v)
    slope = 0.5 * (1.0 + tanh_v) + 0.5 * pre * (1.0 - tanh_v * tanh_v) * 0.7978845608 * (
        1.0 + 3.0 * 0.044715 * pre * pre
    )
    return (value, slope)


def tile_of(size, most):
    return size if size <= most else most


def kernel(
    n, group,
    tokens, cotangent, prob, slot_row, slot_column, keep, w_in, w_out,
    mixed, grad_in, grad_out,
    sent, sent_grad, back,
    weight_in, weight_out, rows_x, rows_g, rows_o, hidden, factor, dpre,
    give_out, came_out, came_in,
    weight_sem, own_sem, x_send, x_recv, g_send, g_recv, o_send, o_recv, pair_send, pair_recv, done_sem,
):
    me = lax.axis_index("expert")
    core = lax.axis_index("replica")
    other = 1 - core
    cap, width = rows_x.shape[1:]
    ff = weight_in.shape[1]
    rows = group * cap
    groups = n // group
    tile = tile_of(ff, 512)
    wide = tile_of(width, 256)
    count = tokens.shape[0]
    give_in = factor.at[pl.ds(0, came_in.shape[0])]

    def weight_copy(i):
        source, target = ((w_in, weight_in), (w_out, weight_out))[i]
        return pltpu.make_async_copy(source, target, weight_sem.at[i])

    weight_copy(0).start()
    weight_copy(1).start()

    def own_copy(i):
        source, target = (
            (sent.at[0], rows_x.at[0]), (sent_grad.at[0], rows_g.at[0]), (rows_o.at[0], back.at[me])
        )[i]
        return pltpu.make_async_copy(source, target, own_sem.at[i])

    def ahead(k):
        return lax.rem(me + k, n)

    def behind(k):
        return lax.rem(me - k + n, n)

    def x_copy(k):
        return pltpu.make_async_remote_copy(
            src_ref=sent.at[k], dst_ref=rows_x.at[k], send_sem=x_send.at[k],
            recv_sem=x_recv.at[k], device_id=(ahead(k), core), device_id_type=MESH,
        )

    def g_copy(k):
        return pltpu.make_async_remote_copy(
            src_ref=sent_grad.at[k], dst_ref=rows_g.at[k], send_sem=g_send.at[k],
            recv_sem=g_recv.at[k], device_id=(ahead(k), core), device_id_type=MESH,
        )

    def o_copy(k):
        return pltpu.make_async_remote_copy(
            src_ref=rows_o.at[k], dst_ref=back.at[me], send_sem=o_send.at[k],
            recv_sem=o_recv.at[k], device_id=(behind(k), core), device_id_type=MESH,
        )

    def pair_copy(i):
        source, target = ((give_out, came_out), (give_in, came_in))[i]
        return pltpu.make_async_remote_copy(
            src_ref=source, dst_ref=target, send_sem=pair_send.at[i],
            recv_sem=pair_recv.at[i], device_id=(me, other), device_id_type=MESH,
        )

    def result_copy(i):
        source, target = ((came_out, grad_out), (came_in, grad_in))[i]
        return pltpu.make_async_copy(source, target, done_sem.at[i])

    def each(low, high, step):
        def run(i, carry):
            step(i)
            return carry

        lax.fori_loop(low, high, run, 0)

    barrier = pltpu.get_barrier_semaphore()

    def greet(k):
        pl.semaphore_signal(barrier, inc=1, device_id=(ahead(k), core), device_id_type=MESH)

    each(1, n, greet)
    pl.semaphore_signal(barrier, inc=1, device_id=(me, other), device_id_type=MESH)

    def dispatch(values, slots):
        def fill(g):
            first = g * group
            shape = (group, cap, count)
            expert = lax.broadcasted_iota(jnp.int32, shape, 0) + (first + me)
            expert = jnp.where(expert >= n, expert - n, expert)
            place = expert * cap + lax.broadcasted_iota(jnp.int32, shape, 1)
            chosen = jnp.where(place == slot_row[...][None], 1.0, 0.0).astype(jnp.bfloat16)
            filled = jnp.dot(
                chosen.reshape(rows, count), values[...], preferred_element_type=jnp.float32
            )
            slots[pl.ds(first, group)] = filled.astype(jnp.bfloat16).reshape(group, cap, width)

        each(0, groups, fill)

    def later(copy):
        def start(i):
            k = lax.rem((1 - core) * (i + n // 4) + core * (n // 4 * 3 - 1 - i + n), n)

            @pl.when(k > 0)
            def _():
                copy(k).start()

        return start

    dispatch(tokens, sent)
    own_copy(0).start()
    pl.semaphore_wait(barrier, n)
    each(0, n, later(x_copy))
    mixed[...] = (prob[...] * cotangent[...].astype(jnp.float32)).astype(jnp.bfloat16)
    dispatch(mixed, sent_grad)
    own_copy(1).start()
    each(0, n, later(g_copy))
    own_copy(0).wait()
    own_copy(1).wait()
    weight_copy(0).wait()
    weight_copy(1).wait()

    def span(first):
        return pl.ds(pl.multiple_of(first * cap, rows), rows)

    def forward(g):
        first = lax.rem((1 - core) * (g + groups // 4) + core * (groups // 4 * 3 - 1 - g + groups), groups) * group

        def arrived(k):
            @pl.when(k > 0)
            def _():
                x_copy(k).wait_recv()

        each(first, first + group, arrived)

        def project(j):
            columns = pl.ds(pl.multiple_of(j * tile, tile), tile)
            block = rows_x[pl.ds(first, group)].reshape(rows, width)
            pre = jnp.dot(block, weight_in[:, columns], preferred_element_type=jnp.float32)
            value, slope = gelu_parts(pre)
            scale = keep[pl.ds(first, group), :, columns]
            value = value.reshape(group, cap, tile) * scale
            slope = slope.reshape(group, cap, tile) * scale
            hidden[pl.ds(first, group), :, columns] = value.astype(jnp.bfloat16)
            factor[span(first), columns] = slope.reshape(rows, tile)

        each(0, ff // tile, project)

        def output(j):
            columns = pl.ds(pl.multiple_of(j * wide, wide), wide)
            block = hidden[pl.ds(first, group)].reshape(rows, ff)
            out = jnp.dot(block, weight_out[:, columns], preferred_element_type=jnp.float32)
            rows_o[pl.ds(first, group), :, columns] = out.astype(jnp.bfloat16).reshape(group, cap, wide)

        each(0, width // wide, output)

        def give_back(k):
            @pl.when(k > 0)
            def _():
                o_copy(k).start()

            @pl.when(k == 0)
            def _():
                own_copy(2).start()

        each(first, first + group, give_back)

    each(0, groups, forward)

    def backward(g):
        first = lax.rem((1 - core) * (g + groups // 4) + core * (groups // 4 * 3 - 1 - g + groups), groups) * group

        def arrived(k):
            @pl.when(k > 0)
            def _():
                g_copy(k).wait_recv()

        each(first, first + group, arrived)

        def pull(j):
            columns = pl.ds(pl.multiple_of(j * tile, tile), tile)
            block = rows_g[pl.ds(first, group)].reshape(rows, width)
            dhidden = lax.dot_general(
                block, weight_out[columns, :], (((1,), (1,)), ((), ())),
                preferred_element_type=jnp.float32,
            )
            dhidden = (dhidden * factor[span(first), columns]).astype(jnp.bfloat16)
            dpre[pl.ds(first, group), :, columns] = dhidden.reshape(group, cap, tile)

        each(0, ff // tile, pull)

    each(0, groups, backward)

    def product(left, right, start, j, part):
        columns = pl.ds(pl.multiple_of(start + j * part, part), part)
        return lax.dot_general(
            left[:, :, columns].reshape(n * cap, part), right[...].reshape(n * cap, right.shape[2]),
            (((0,), (0,)), ((), ())), preferred_element_type=jnp.float32,
        )

    def gradient(i, left, right, give, came):
        half = give.shape[0]
        part = tile_of(half, 256)

        def theirs(j):
            give[pl.ds(pl.multiple_of(j * part, part), part), :] = product(
                left, right, other * half, j, part)

        def mine(j):
            spot = pl.ds(pl.multiple_of(j * part, part), part)
            came[spot, :] += product(left, right, core * half, j, part)

        return functools.partial(each, 0, half // part, theirs), functools.partial(each, 0, half // part, mine)

    theirs_out, mine_out = gradient(0, hidden, rows_g, give_out, came_out)
    theirs_in, mine_in = gradient(1, rows_x, dpre, give_in, came_in)
    theirs_out()
    pair_copy(0).start()
    theirs_in()
    pair_copy(1).start()
    pair_copy(0).wait_recv()
    mine_out()
    result_copy(0).start()
    pair_copy(1).wait_recv()
    mine_in()
    result_copy(1).start()

    own_copy(2).wait()

    def finish(k):
        x_copy(k).wait_send()
        g_copy(k).wait_send()
        o_copy(k).wait_send()

    each(1, n, lambda k: o_copy(k).wait_recv())

    def combine(j):
        columns = pl.ds(pl.multiple_of(j * wide, wide), wide)
        place = lax.broadcasted_iota(jnp.int32, (count, n * cap), 1)
        chosen = jnp.where(place == slot_column[...], 1.0, 0.0).astype(jnp.bfloat16)
        out = jnp.dot(
            chosen, back[:, :, columns].reshape(n * cap, wide), preferred_element_type=jnp.float32
        )
        mixed[:, columns] = (prob[...] * out).astype(jnp.bfloat16)

    each(0, width // wide, combine)
    each(1, n, finish)
    pair_copy(0).wait_send()
    pair_copy(1).wait_send()
    result_copy(0).wait()
    result_copy(1).wait()


def exchange(n, cap, tokens, cotangent, prob, target, keep, w_in, w_out):
    count, width = tokens.shape
    ff = w_in.shape[1]
    group = min(n, max(1, 256 // cap))
    dma = pltpu.SemaphoreType.DMA
    f32, bf16 = jnp.float32, jnp.bfloat16
    whole = pl.BlockSpec(memory_space=pl.ANY)
    flops = 10 * n * cap * width * ff
    return pl.pallas_call(
        functools.partial(kernel, n, group),
        out_shape=(
            jax.ShapeDtypeStruct((count, width), bf16),
            jax.ShapeDtypeStruct((width // 2, ff), f32),
            jax.ShapeDtypeStruct((ff // 2, width), f32),
        ),
        in_specs=[pl.BlockSpec(memory_space=pltpu.VMEM)] * 6 + [whole, whole],
        out_specs=(pl.BlockSpec(memory_space=pltpu.VMEM), whole, whole),
        scratch_shapes=[
            pltpu.VMEM((n, cap, width), bf16),
            pltpu.VMEM((n, cap, width), bf16),
            pltpu.VMEM((n, cap, width), bf16),
            pltpu.VMEM((width, ff), bf16),
            pltpu.VMEM((ff, width), bf16),
            pltpu.VMEM((n, cap, width), bf16),
            pltpu.VMEM((n, cap, width), bf16),
            pltpu.VMEM((n, cap, width), bf16),
            pltpu.VMEM((n, cap, ff), bf16),
            pltpu.VMEM((n * cap, ff), f32),
            pltpu.VMEM((n, cap, ff), bf16),
            pltpu.VMEM((ff // 2, width), f32),
            pltpu.VMEM((ff // 2, width), f32),
            pltpu.VMEM((width // 2, ff), f32),
            dma((2,)), dma((3,)), dma((n,)), dma((n,)), dma((n,)), dma((n,)), dma((n,)), dma((n,)),
            dma((2,)), dma((2,)), dma((2,)),
        ],
        cost_estimate=pl.CostEstimate(flops=flops, bytes_accessed=40 << 20, transcendentals=n * cap * ff),
        compiler_params=pltpu.CompilerParams(
            collective_id=0, has_side_effects=True, vmem_limit_bytes=67043328
        ),
    )(tokens, cotangent, prob[:, None], target[None, :], target[:, None], keep, w_in, w_out)


def shards(tokens, expert_id, router_prob, keep_mask, w_in, w_out, cotangent):
    tok_rows, width = tokens.shape
    n_expert = lax.axis_size("expert")
    n_replica = lax.axis_size("replica")
    capacity = 2 * tok_rows // n_expert
    portion = capacity // n_replica
    weight_in = w_in[0]
    weight_out = w_out[0]
    ids = expert_id[:, 0]
    onehot = (ids[:, None] == jnp.arange(n_expert, dtype=jnp.int32)[None, :]).astype(jnp.int32)
    ranks = jnp.sum(jnp.cumsum(onehot, axis=0) * onehot, axis=1) - 1
    target = ids * capacity + ranks % n_replica * portion + ranks // n_replica
    keep_rows = lax.dynamic_index_in_dim(
        keep_mask[0].reshape(n_expert, n_replica, -1),
        lax.axis_index("replica"),
        axis=1,
        keepdims=False,
    )
    keep_scale = keep_rows.astype(jnp.float32) * KEEP_SCALE
    sources = (lax.axis_index("expert") - jnp.arange(n_expert) + n_expert) % n_expert
    keep_scale = keep_scale[sources][:, None, :]
    mixed, grad_in, grad_out = exchange(
        n_expert, capacity, tokens, cotangent, router_prob, target, keep_scale, weight_in, weight_out
    )
    return (mixed, grad_in[None], grad_out[None])


def solution(mesh):
    in_specs = (
        P(("expert", "replica"), None),
        P(("expert", "replica"), None),
        P(("expert", "replica")),
        P("expert", None, None),
        P("expert", None, None),
        P("expert", None, None),
        P(("expert", "replica"), None),
    )
    out_specs = (
        P(("expert", "replica"), None),
        P("expert", "replica", None),
        P("expert", "replica", None),
    )
    return jax.shard_map(shards, mesh=mesh, in_specs=in_specs, out_specs=out_specs, check_vma=False)
```

profile of v0, /device:TPU:0, one launch (start us, length us, event | category | flops | bytes accessed | tf_op | source)
XLA Modules:
  0.0 169.7 jit_solution(8668759913019401630)
XLA Ops:
  0.7 0.7 fusion.11
  1.4 1.1 reduce-window.6
  2.5 0.2 slice_reduce_fusion
  2.7 0.8 fusion.10
  3.5 0.1 copy.13
  3.7 1.5 copy.18.prob
  5.2 1.1 reshape_squeeze.3
  6.3 0.1 constant_dynamic-slice_fusion
  6.5 0.1 fusion.8
  6.5 0.6 gather_fusion
  7.1 0.7 broadcast_in_dim.17.keep
  7.9 0.8 copy.11
  8.7 1.0 fusion.2
  9.7 0.6 fusion.14.slot_row
  10.3 150.2 %shard_map.94 = (bf16[512,1024]{1,0:T(8,128)(2,1)}, f32[512,2048]{1,0:T(8,128)}, f32[1024,1024]{1,0:T(8,128)}) custom-call(bf16[512,1024]{1,0:T(8,128)(2,1)} %tokens.1, bf16[512,1024]{1,0:T(8,128)(2,1)} %cotangent.1, f32[512,1]{1,0:T(8,128)} %copy.18.prob, s32[1,512]{1,0:T(1,128)} %fusion.14.slot_row, s32[512,1]{1,0:T(8,128)} %get-tuple-element.9.slot_column, ...), custom_call_target="tpu_custom_call" | custom-call | flops 21474836480 | bytes 41943040 | tf_op jit(solution)/shard_map/pallas_call | solution.py:289
  160.5 2.3 %copy.30 = bf16[512,1024]{1,0:T(8,128)(2,1)} copy(bf16[512,1024]{1,0:T(8,128)(2,1)} %get-tuple-element.14) | data formatting | bytes 2097152
  162.8 0.0 copy-start
  162.8 4.8 %copy.31 = f32[1,512,2048]{2,1,0:T(8,128)} copy(f32[1,512,2048]{2,1,0:T(8,128)} %bitcast.30) | data formatting | bytes 8388608
  167.6 0.0 copy-done
  167.6 2.0 %copy.32 = f32[1,1024,1024]{2,1,0:T(8,128)} copy(f32[1,1024,1024]{2,1,0:T(8,128)S(1)} %bitcast.29) | data formatting | bytes 8388608
  (5 shorter events, 0.1 us)
Async XLA Ops:
  162.8 4.9 %copy-start = (f32[1024,1024]{1,0:T(8,128)S(1)}, f32[1024,1024]{1,0:T(8,128)}, u32[]{:S(2)}) copy-start(f32[1024,1024]{1,0:T(8,128)} %get-tuple-element.8) | copy-start | bytes 12582916
where the time goes:
time: 170 us
  Pallas kernels  150 us (88%)
  local copies, waits for them, and re-layouts  14.4 us (8%)
  other arithmetic  4.31 us (3%)
    pallas_call x1, Pallas kernels, exchange(): pl.pallas_call(functools.partial(kernel, n, group), out_shape=(jax.ShapeD...  150 us
    unnamed x6, local copies, waits for them, and re-layouts  9.95 us

commit v1 on v0

v1 whole, which is shorter than its diff:
```python
import functools

import jax
import jax.numpy as jnp
from jax import lax
from jax.experimental import pallas as pl
from jax.experimental.pallas import tpu as pltpu
from jax.sharding import PartitionSpec as P

KEEP_SCALE = 4.0 / 3.0
MESH = pl.DeviceIdType.MESH


def gelu_parts(pre):
    inner = 0.7978845608 * (pre + 0.044715 * pre * pre * pre)
    tanh_v = jnp.tanh(inner)
    value = 0.5 * pre * (1.0 + tanh_v)
    slope = 0.5 * (1.0 + tanh_v) + 0.5 * pre * (1.0 - tanh_v * tanh_v) * 0.7978845608 * (
        1.0 + 3.0 * 0.044715 * pre * pre
    )
    return (value, slope)


def tile_of(size, most):
    return size if size <= most else most


def each(low, high, step):
    def run(i, carry):
        step(i)
        return carry

    lax.fori_loop(low, high, run, 0)


def kernel(
    n, shifts,
    ids, prob, tokens, cotangent, keep, w_in, w_out,
    mixed, grad_in, grad_out,
    own_x, own_g, keep_raw, keep_rows, slot, columns_of,
    sent, sent_grad, back,
    weight_in, weight_out, rows_x, rows_g, rows_o, hidden, factor, dpre,
    give_out, give_in, came_out, came_in,
    load_sem, own_sem, x_send, x_recv, g_send, g_recv, o_send, o_recv, pair_send, pair_recv,
):
    me = lax.axis_index("expert")
    core = lax.axis_index("replica")
    other = 1 - core
    group = n // shifts
    plane = me // group
    spot = lax.rem(me, group)
    cap, width = rows_x.shape[1:]
    ff = weight_in.shape[1]
    rows = group * cap
    tile = tile_of(ff, 512)
    wide = tile_of(width, 256)
    count = own_x.shape[0]
    total = factor.at[pl.ds(0, count), pl.ds(0, width)]

    def load(i):
        source, target = (
            (tokens, own_x), (cotangent, own_g), (keep, keep_raw), (w_in, weight_in), (w_out, weight_out)
        )[i]
        return pltpu.make_async_copy(source, target, load_sem.at[i])

    for i in range(5):
        load(i).start()

    def ahead(shift, turn):
        return lax.rem(plane + shift, shifts) * group + lax.rem(spot + turn, group)

    def behind(shift, turn):
        return lax.rem(plane - shift + shifts, shifts) * group + lax.rem(spot - turn + group, group)

    def x_copy(shift, turn):
        k = shift * group + turn
        return pltpu.make_async_remote_copy(
            src_ref=sent.at[k], dst_ref=rows_x.at[k], send_sem=x_send.at[k],
            recv_sem=x_recv.at[k], device_id=(ahead(shift, turn), core), device_id_type=MESH,
        )

    def g_copy(shift, turn):
        k = shift * group + turn
        return pltpu.make_async_remote_copy(
            src_ref=sent_grad.at[k], dst_ref=rows_g.at[k], send_sem=g_send.at[k],
            recv_sem=g_recv.at[k], device_id=(ahead(shift, turn), core), device_id_type=MESH,
        )

    def o_copy(shift, turn):
        k = shift * group + turn
        return pltpu.make_async_remote_copy(
            src_ref=rows_o.at[k], dst_ref=back.at[k], send_sem=o_send.at[k],
            recv_sem=o_recv.at[k], device_id=(behind(shift, turn), core), device_id_type=MESH,
        )

    def own_copy(i):
        source, target = (
            (sent.at[0], rows_x.at[0]), (sent_grad.at[0], rows_g.at[0]), (rows_o.at[0], back.at[0])
        )[i]
        return pltpu.make_async_copy(source, target, own_sem.at[i])

    def pair_copy(i):
        source, target = ((give_out, came_out), (give_in, came_in))[i]
        return pltpu.make_async_remote_copy(
            src_ref=source, dst_ref=target, send_sem=pair_send.at[i],
            recv_sem=pair_recv.at[i], device_id=(me, other), device_id_type=MESH,
        )

    def blocks(shift, step):
        def one(turn):
            @pl.when(shift * group + turn > 0)
            def _():
                step(shift, turn)

        each(0, group, one)

    barrier = pltpu.get_barrier_semaphore()

    def greet(shift, turn):
        pl.semaphore_signal(barrier, inc=1, device_id=(ahead(shift, turn), core), device_id_type=MESH)

    each(0, shifts, lambda shift: blocks(shift, greet))
    pl.semaphore_signal(barrier, inc=1, device_id=(me, other), device_id_type=MESH)

    low = plane * 2 < shifts
    even = lax.rem(plane, 2) == 0

    def send_order(i):
        return jnp.where(low, lax.rem(i + 1, shifts), lax.rem(shifts - 1 - i + shifts, shifts))

    def near_first(i, sign):
        first = jnp.where(even, shifts - 1, 1)
        last = (plane + 3) // 2
        place = jnp.where(i == 0, 0, jnp.where(i == 1, first, jnp.where(i == 3, last, 6 - first - last)))
        if shifts != 4:
            place = i
        return place if sign > 0 else lax.rem(shifts - place, shifts)

    expert_rows = lax.broadcasted_iota(jnp.int32, (n, count), 0)
    hot = jnp.where(expert_rows == ids[...], 1.0, 0.0)
    before = lax.broadcasted_iota(jnp.int32, (count, count), 0) <= lax.broadcasted_iota(
        jnp.int32, (count, count), 1)
    counted = jnp.dot(
        hot.astype(jnp.bfloat16), jnp.where(before, 1.0, 0.0).astype(jnp.bfloat16),
        preferred_element_type=jnp.float32,
    )
    rank = jnp.sum(hot * counted, axis=0, keepdims=True) - 1.0
    place_of = ids[...] * cap + rank.astype(jnp.int32)
    slot[...] = place_of
    pair = lax.broadcasted_iota(jnp.int32, (128, count), 0) == 0
    columns_of[...] = jnp.transpose(jnp.where(pair, place_of.astype(jnp.float32), prob[...]))

    def dispatch(values, slots, shift):
        shape = (group, cap, count)
        turn = lax.broadcasted_iota(jnp.int32, shape, 0) + spot
        turn = jnp.where(turn >= group, turn - group, turn)
        place = (lax.rem(plane + shift, shifts) * group + turn) * cap + lax.broadcasted_iota(jnp.int32, shape, 1)
        chosen = jnp.where(place == slot[...][None], 1.0, 0.0).astype(jnp.bfloat16)
        filled = jnp.dot(
            chosen.reshape(rows, count), values[...], preferred_element_type=jnp.float32
        )
        slots[pl.ds(shift * group, group)] = filled.astype(jnp.bfloat16).reshape(group, cap, width)

    def start(copy):
        return lambda shift, turn: copy(shift, turn).start()

    load(0).wait()
    dispatch(own_x, sent, send_order(0))
    pl.semaphore_wait(barrier, n)

    def send_x(i):
        dispatch(own_x, sent, send_order(i))
        blocks(send_order(i - 1), start(x_copy))

    each(1, shifts, send_x)
    load(1).wait()
    own_g[...] = (columns_of[:, 1:2] * own_g[...].astype(jnp.float32)).astype(jnp.bfloat16)
    blocks(send_order(shifts - 1), start(x_copy))
    own_copy(0).start()

    def send_g(i):
        dispatch(own_g, sent_grad, send_order(i))

        @pl.when(i > 0)
        def _():
            blocks(send_order(i - 1), start(g_copy))

    each(0, shifts, send_g)
    load(2).wait()

    def keep_row(k):
        source = behind(k // group, lax.rem(k, group)) * 2 + core
        keep_rows[k] = keep_raw[pl.ds(source, 1), :].astype(jnp.float32) * KEEP_SCALE

    each(0, n, keep_row)
    blocks(send_order(shifts - 1), start(g_copy))
    own_copy(1).start()
    own_copy(0).wait()
    own_copy(1).wait()
    load(3).wait()
    load(4).wait()

    def forward(i):
        shift = near_first(i, 1)
        first = shift * group
        span = pl.ds(pl.multiple_of(first * cap, rows), rows)
        blocks(shift, lambda s, t: x_copy(s, t).wait_recv())

        def project(j):
            columns = pl.ds(pl.multiple_of(j * tile, tile), tile)
            block = rows_x[pl.ds(first, group)].reshape(rows, width)
            pre = jnp.dot(block, weight_in[:, columns], preferred_element_type=jnp.float32)
            value, slope = gelu_parts(pre)
            scale = keep_rows[pl.ds(first, group), :, columns]
            value = value.reshape(group, cap, tile) * scale
            slope = slope.reshape(group, cap, tile) * scale
            hidden[pl.ds(first, group), :, columns] = value.astype(jnp.bfloat16)
            factor[span, columns] = slope.reshape(rows, tile)

        each(0, ff // tile, project)

        def output(j):
            columns = pl.ds(pl.multiple_of(j * wide, wide), wide)
            block = hidden[pl.ds(first, group)].reshape(rows, ff)
            out = jnp.dot(block, weight_out[:, columns], preferred_element_type=jnp.float32)
            rows_o[pl.ds(first, group), :, columns] = out.astype(jnp.bfloat16).reshape(group, cap, wide)

        each(0, width // wide, output)
        blocks(shift, start(o_copy))

        @pl.when(shift == 0)
        def _():
            own_copy(2).start()

    each(0, shifts, forward)

    def backward(i):
        shift = near_first(i, 1)
        first = shift * group
        span = pl.ds(pl.multiple_of(first * cap, rows), rows)
        blocks(shift, lambda s, t: g_copy(s, t).wait_recv())

        def pull(j):
            columns = pl.ds(pl.multiple_of(j * tile, tile), tile)
            block = rows_g[pl.ds(first, group)].reshape(rows, width)
            dhidden = lax.dot_general(
                block, weight_out[columns, :], (((1,), (1,)), ((), ())),
                preferred_element_type=jnp.float32,
            )
            dhidden = (dhidden * factor[span, columns]).astype(jnp.bfloat16)
            dpre[pl.ds(first, group), :, columns] = dhidden.reshape(group, cap, tile)

        each(0, ff // tile, pull)

    each(0, shifts, backward)

    def product(left, right, first, j, part):
        columns = pl.ds(pl.multiple_of(first + j * part, part), part)
        return lax.dot_general(
            left[:, :, columns].reshape(n * cap, part), right[...].reshape(n * cap, right.shape[2]),
            (((0,), (0,)), ((), ())), preferred_element_type=jnp.float32,
        )

    def gradient(left, right, give, came, result):
        half = give.shape[0]
        part = tile_of(half, 256)

        def theirs(j):
            give[pl.ds(pl.multiple_of(j * part, part), part), :] = product(
                left, right, other * half, j, part).astype(jnp.bfloat16)

        def mine(j):
            band = pl.ds(pl.multiple_of(j * part, part), part)
            result[band, :] = came[band, :].astype(jnp.float32) + product(left, right, core * half, j, part)

        return functools.partial(each, 0, half // part, theirs), functools.partial(each, 0, half // part, mine)

    theirs_out, mine_out = gradient(hidden, rows_g, give_out, came_out, grad_out)
    theirs_in, mine_in = gradient(rows_x, dpre, give_in, came_in, grad_in)
    theirs_out()
    pair_copy(0).start()
    theirs_in()
    pair_copy(1).start()
    pair_copy(0).wait_recv()
    mine_out()
    pair_copy(1).wait_recv()
    mine_in()
    pair_copy(0).wait_send()
    own_copy(2).wait()

    def chosen_of(shift):
        lane = lax.broadcasted_iota(jnp.int32, (count, rows), 1)
        turn = lane // cap + spot
        turn = jnp.where(turn >= group, turn - group, turn)
        place = (lax.rem(plane + shift, shifts) * group + turn) * cap + lax.rem(lane, cap)
        return jnp.where(place == columns_of[:, 0:1].astype(jnp.int32), 1.0, 0.0).astype(jnp.bfloat16)

    def part_of(chosen, shift, columns):
        return jnp.dot(
            chosen, back[pl.ds(shift * group, group), :, columns].reshape(rows, wide),
            preferred_element_type=jnp.float32,
        )

    def combine(i):
        shift = near_first(i, -1)
        chosen = chosen_of(shift)
        blocks(shift, lambda s, t: o_copy(s, t).wait_recv())
        for j in range(width // wide):
            columns = pl.ds(j * wide, wide)
            added = part_of(chosen, shift, columns)

            @pl.when(i == 0)
            def _():
                total[:, columns] = added

            @pl.when(i > 0)
            def _():
                total[:, columns] += added

    each(0, shifts - 1, combine)

    def finish(shift, turn):
        x_copy(shift, turn).wait_send()
        g_copy(shift, turn).wait_send()

    each(0, shifts, lambda shift: blocks(shift, finish))
    pair_copy(1).wait_send()
    shift = near_first(shifts - 1, -1)
    chosen = chosen_of(shift)
    blocks(shift, lambda s, t: o_copy(s, t).wait_recv())
    for j in range(width // wide):
        columns = pl.ds(j * wide, wide)
        added = part_of(chosen, shift, columns)
        mixed[:, columns] = (columns_of[:, 1:2] * (total[:, columns] + added)).astype(jnp.bfloat16)
    each(0, shifts, lambda shift: blocks(shift, lambda s, t: o_copy(s, t).wait_send()))


def exchange(n, cap, ids, prob, tokens, cotangent, keep, w_in, w_out):
    count, width = tokens.shape
    ff = w_in.shape[1]
    shifts = 4 if n % 4 == 0 else 1
    dma = pltpu.SemaphoreType.DMA
    f32, bf16 = jnp.float32, jnp.bfloat16
    whole = pl.BlockSpec(memory_space=pl.ANY)
    near = pl.BlockSpec(memory_space=pltpu.VMEM)
    flops = 10 * n * cap * width * ff
    return pl.pallas_call(
        functools.partial(kernel, n, shifts),
        out_shape=(
            pltpu.VMEM((count, width), bf16),
            pltpu.VMEM((width // 2, ff), f32),
            pltpu.VMEM((ff // 2, width), f32),
        ),
        in_specs=[near] * 2 + [whole] * 5,
        out_specs=(near, near, near),
        scratch_shapes=[
            pltpu.VMEM((count, width), bf16),
            pltpu.VMEM((count, width), bf16),
            pltpu.VMEM(keep.shape, jnp.int32),
            pltpu.VMEM((n, 1, ff), f32),
            pltpu.VMEM((1, count), jnp.int32),
            pltpu.VMEM((count, 128), f32),
            pltpu.VMEM((n, cap, width), bf16),
            pltpu.VMEM((n, cap, width), bf16),
            pltpu.VMEM((n, cap, width), bf16),
            pltpu.VMEM((width, ff), bf16),
            pltpu.VMEM((ff, width), bf16),
            pltpu.VMEM((n, cap, width), bf16),
            pltpu.VMEM((n, cap, width), bf16),
            pltpu.VMEM((n, cap, width), bf16),
            pltpu.VMEM((n, cap, ff), bf16),
            pltpu.VMEM((n * cap, ff), f32),
            pltpu.VMEM((n, cap, ff), bf16),
            pltpu.VMEM((ff // 2, width), bf16),
            pltpu.VMEM((width // 2, ff), bf16),
            pltpu.VMEM((ff // 2, width), bf16),
            pltpu.VMEM((width // 2, ff), bf16),
            dma((5,)), dma((3,)), dma((n,)), dma((n,)), dma((n,)), dma((n,)), dma((n,)), dma((n,)),
            dma((2,)), dma((2,)),
        ],
        cost_estimate=pl.CostEstimate(flops=flops, bytes_accessed=40 << 20, transcendentals=n * cap * ff),
        compiler_params=pltpu.CompilerParams(
            collective_id=0, has_side_effects=True, vmem_limit_bytes=52 << 20
        ),
    )(ids, prob, tokens, cotangent, keep, w_in, w_out)


def shards(tokens, expert_id, router_prob, keep_mask, w_in, w_out, cotangent):
    count = tokens.shape[0]
    n = lax.axis_size("expert")
    mixed, grad_in, grad_out = exchange(
        n, 2 * count // n, expert_id.reshape(1, count), router_prob.reshape(1, count),
        tokens, cotangent, keep_mask[0], w_in[0], w_out[0],
    )
    return (mixed, grad_in[None], grad_out[None])


def solution(mesh):
    in_specs = (
        P(("expert", "replica"), None),
        P(("expert", "replica"), None),
        P(("expert", "replica")),
        P("expert", None, None),
        P("expert", None, None),
        P("expert", None, None),
        P(("expert", "replica"), None),
    )
    out_specs = (
        P(("expert", "replica"), None),
        P("expert", "replica", None),
        P("expert", "replica", None),
    )
    return jax.shard_map(shards, mesh=mesh, in_specs=in_specs, out_specs=out_specs, check_vma=False)
```

time: 170 us -> 158 us (0.929)
  local copies, waits for them, and re-layouts: 14.4 us -> 5 us
  other arithmetic: 4.31 us -> 0 us
  Pallas kernels: 150 us -> 152 us
    unnamed x6 -> x3, local copies, waits for them, and re-layouts: 9.95 us -> 5 us
    broadcast_in_dim x2 -> x0, local copies, waits for them, and re-layouts: 2.29 us -> none  [the longest x1 1.54 us: exchange(): prob[:, None]]
where the time goes in v1:
time: 158 us; the launch traced here: 157 us
  Pallas kernels  152 us (96%)
  local copies, waits for them, and re-layouts  5 us (3%)
    pallas_call x1, Pallas kernels, exchange(): pl.pallas_call(functools.partial(kernel, n, shifts), out_shape=(pltpu.VME...  152 us
    unnamed x3, local copies, waits for them, and re-layouts  5 us

profile of v1, /device:TPU:0, one launch (start us, length us, event | category | flops | bytes accessed | tf_op | source)
XLA Modules:
  0.0 157.3 jit_solution(6978503325782278051)
XLA Ops:
  0.6 151.7 %shard_map.94 = (bf16[512,1024]{1,0:T(8,128)(2,1)S(1)}, f32[512,2048]{1,0:T(8,128)S(1)}, f32[1024,1024]{1,0:T(8,128)S(1)}) custom-call(s32[1,512]{1,0:T(1,128)} %bitcast.12, f32[1,512]{1,0:T(1,128)} %bitcast.13, bf16[512,1024]{1,0:T(8,128)(2,1)} %tokens.1, bf16[512,1024]{1,0:T(8,128)(2,1)} %cotangent.1, s32[32,2048]{1,0:T(8,128)} %bitcast.11, ...), custom_call_target="tpu_custom_call" | custom-call | flops 21474836480 | bytes 41943040 | tf_op jit(solution)/shard_map/pallas_call | solution.py:347
  152.3 1.0 copy.13
  153.3 2.0 %copy.14 = f32[1,512,2048]{2,1,0:T(8,128)} copy(f32[1,512,2048]{2,1,0:T(8,128)S(1)} %bitcast.8) | data formatting | bytes 8388608
  155.3 2.0 %copy.15 = f32[1,1024,1024]{2,1,0:T(8,128)} copy(f32[1,1024,1024]{2,1,0:T(8,128)S(1)} %bitcast.7) | data formatting | bytes 8388608

commit v2 on v1

--- a/solution.py
+++ b/solution.py
@@ -35,9 +35,9 @@
 
 def kernel(
     n, shifts,
-    ids, prob, tokens, cotangent, keep, w_in, w_out,
+    ids_in, prob_in, tokens, cotangent, keep, w_in, w_out,
     mixed, grad_in, grad_out,
-    own_x, own_g, keep_raw, keep_rows, slot, columns_of,
+    ids, prob, own_x, own_g, keep_raw, keep_rows, slot, columns_of,
     sent, sent_grad, back,
     weight_in, weight_out, rows_x, rows_g, rows_o, hidden, factor, dpre,
     give_out, give_in, came_out, came_in,
@@ -59,12 +59,14 @@
 
     def load(i):
         source, target = (
-            (tokens, own_x), (cotangent, own_g), (keep, keep_raw), (w_in, weight_in), (w_out, weight_out)
+            (tokens, own_x), (cotangent, own_g), (keep, keep_raw), (w_in, weight_in), (w_out, weight_out),
+            (ids_in, ids), (prob_in, prob),
         )[i]
         return pltpu.make_async_copy(source, target, load_sem.at[i])
 
-    for i in range(5):
-        load(i).start()
+    load(5).start()
+    load(6).start()
+    load(0).start()
 
     def ahead(shift, turn):
         return lax.rem(plane + shift, shifts) * group + lax.rem(spot + turn, group)
@@ -136,6 +138,8 @@
             place = i
         return place if sign > 0 else lax.rem(shifts - place, shifts)
 
+    load(5).wait()
+    load(6).wait()
     expert_rows = lax.broadcasted_iota(jnp.int32, (n, count), 0)
     hot = jnp.where(expert_rows == ids[...], 1.0, 0.0)
     before = lax.broadcasted_iota(jnp.int32, (count, count), 0) <= lax.broadcasted_iota(
@@ -165,27 +169,28 @@
         return lambda shift, turn: copy(shift, turn).start()
 
     load(0).wait()
-    dispatch(own_x, sent, send_order(0))
-    pl.semaphore_wait(barrier, n)
-
+    for i in range(1, 5):
+        load(i).start()
     def send_x(i):
         dispatch(own_x, sent, send_order(i))
-        blocks(send_order(i - 1), start(x_copy))
-
-    each(1, shifts, send_x)
+
+        @pl.when(i == 0)
+        def _():
+            pl.semaphore_wait(barrier, n)
+
+        blocks(send_order(i), start(x_copy))
+
+    each(0, shifts, send_x)
+    own_copy(0).start()
     load(1).wait()
     own_g[...] = (columns_of[:, 1:2] * own_g[...].astype(jnp.float32)).astype(jnp.bfloat16)
-    blocks(send_order(shifts - 1), start(x_copy))
-    own_copy(0).start()
 
     def send_g(i):
         dispatch(own_g, sent_grad, send_order(i))
-
-        @pl.when(i > 0)
-        def _():
-            blocks(send_order(i - 1), start(g_copy))
+        blocks(send_order(i), start(g_copy))
 
     each(0, shifts, send_g)
+    own_copy(1).start()
     load(2).wait()
 
     def keep_row(k):
@@ -193,8 +198,6 @@
         keep_rows[k] = keep_raw[pl.ds(source, 1), :].astype(jnp.float32) * KEEP_SCALE
 
     each(0, n, keep_row)
-    blocks(send_order(shifts - 1), start(g_copy))
-    own_copy(1).start()
     own_copy(0).wait()
     own_copy(1).wait()
     load(3).wait()
@@ -226,13 +229,17 @@
             rows_o[pl.ds(first, group), :, columns] = out.astype(jnp.bfloat16).reshape(group, cap, wide)
 
         each(0, width // wide, output)
-        blocks(shift, start(o_copy))
+
+        @pl.when(i < shifts // 2)
+        def _():
+            blocks(shift, start(o_copy))
 
         @pl.when(shift == 0)
         def _():
             own_copy(2).start()
 
     each(0, shifts, forward)
+    each(0, shifts - shifts // 2, lambda i: blocks(near_first(shifts - 1 - i, 1), start(o_copy)))
 
     def backward(i):
         shift = near_first(i, 1)
@@ -288,36 +295,49 @@
     pair_copy(0).wait_send()
     own_copy(2).wait()
 
-    def chosen_of(shift):
-        lane = lax.broadcasted_iota(jnp.int32, (count, rows), 1)
-        turn = lane // cap + spot
-        turn = jnp.where(turn >= group, turn - group, turn)
-        place = (lax.rem(plane + shift, shifts) * group + turn) * cap + lax.rem(lane, cap)
-        return jnp.where(place == columns_of[:, 0:1].astype(jnp.int32), 1.0, 0.0).astype(jnp.bfloat16)
-
-    def part_of(chosen, shift, columns):
-        return jnp.dot(
-            chosen, back[pl.ds(shift * group, group), :, columns].reshape(rows, wide),
-            preferred_element_type=jnp.float32,
-        )
-
-    def combine(i):
-        shift = near_first(i, -1)
-        chosen = chosen_of(shift)
-        blocks(shift, lambda s, t: o_copy(s, t).wait_recv())
+    def merge(pieces, first, last):
+        many = pieces[0][2] * cap
+        lane = lax.broadcasted_iota(jnp.int32, (1, len(pieces) * many), 1)
+        place = jnp.full(lane.shape, -1, jnp.int32)
+        for at, (shift, low_turn, turns) in enumerate(pieces):
+            inside = lane - at * many
+            turn = lax.rem(inside // cap + low_turn + spot, group)
+            found = (lax.rem(plane + shift, shifts) * group + turn) * cap + lax.rem(inside, cap)
+            place = jnp.where((inside >= 0) & (inside < many), found, place)
+        chosen = jnp.where(place == columns_of[:, 0:1].astype(jnp.int32), 1.0, 0.0).astype(jnp.bfloat16)
+        for shift, low_turn, turns in pieces:
+            def arrived(turn):
+                @pl.when(shift * group + turn > 0)
+                def _():
+                    o_copy(shift, turn).wait_recv()
+
+            each(low_turn, low_turn + turns, arrived)
         for j in range(width // wide):
             columns = pl.ds(j * wide, wide)
-            added = part_of(chosen, shift, columns)
-
-            @pl.when(i == 0)
-            def _():
+            block = jnp.concatenate([
+                back[pl.ds(shift * group + low_turn, turns), :, columns].reshape(many, wide)
+                for shift, low_turn, turns in pieces
+            ], axis=0)
+            added = jnp.dot(chosen, block, preferred_element_type=jnp.float32)
+            if not first:
+                added += total[:, columns]
+            if last:
+                mixed[:, columns] = (columns_of[:, 1:2] * added).astype(jnp.bfloat16)
+            else:
                 total[:, columns] = added
 
-            @pl.when(i > 0)
-            def _():
-                total[:, columns] += added
-
-    each(0, shifts - 1, combine)
+    far = [near_first(i, -1) for i in range(2, shifts)]
+    half, quarter = group // 2, group // 4
+    if shifts == 4 and quarter * 4 == group:
+        merge([(0, 0, group)], True, False)
+        merge([(near_first(1, -1), 0, group)], False, False)
+        merge([(shift, 0, half) for shift in far], False, False)
+        merge([(shift, half, quarter) for shift in far], False, False)
+        final = [(shift, half + quarter, quarter) for shift in far]
+    else:
+        for shift in range(shifts - 1):
+            merge([(shift, 0, group)], shift == 0, False)
+        final = [(shifts - 1, 0, group)]
 
     def finish(shift, turn):
         x_copy(shift, turn).wait_send()
@@ -325,13 +345,7 @@
 
     each(0, shifts, lambda shift: blocks(shift, finish))
     pair_copy(1).wait_send()
-    shift = near_first(shifts - 1, -1)
-    chosen = chosen_of(shift)
-    blocks(shift, lambda s, t: o_copy(s, t).wait_recv())
-    for j in range(width // wide):
-        columns = pl.ds(j * wide, wide)
-        added = part_of(chosen, shift, columns)
-        mixed[:, columns] = (columns_of[:, 1:2] * (total[:, columns] + added)).astype(jnp.bfloat16)
+    merge(final, shifts == 1, True)
     each(0, shifts, lambda shift: blocks(shift, lambda s, t: o_copy(s, t).wait_send()))
 
 
@@ -351,9 +365,11 @@
             pltpu.VMEM((width // 2, ff), f32),
             pltpu.VMEM((ff // 2, width), f32),
         ),
-        in_specs=[near] * 2 + [whole] * 5,
+        in_specs=[whole] * 7,
         out_specs=(near, near, near),
         scratch_shapes=[
+            pltpu.VMEM((1, count), jnp.int32),
+            pltpu.VMEM((1, count), f32),
             pltpu.VMEM((count, width), bf16),
             pltpu.VMEM((count, width), bf16),
             pltpu.VMEM(keep.shape, jnp.int32),
@@ -375,7 +391,7 @@
             pltpu.VMEM((width // 2, ff), bf16),
             pltpu.VMEM((ff // 2, width), bf16),
             pltpu.VMEM((width // 2, ff), bf16),
-            dma((5,)), dma((3,)), dma((n,)), dma((n,)), dma((n,)), dma((n,)), dma((n,)), dma((n,)),
+            dma((7,)), dma((3,)), dma((n,)), dma((n,)), dma((n,)), dma((n,)), dma((n,)), dma((n,)),
             dma((2,)), dma((2,)),
         ],
         cost_estimate=pl.CostEstimate(flops=flops, bytes_accessed=40 << 20, transcendentals=n * cap * ff),

time: 158 us -> 152 us (0.962)
  the two profiles are of different devices: /device:TPU:0 before, /device:TPU:18 now
where the time goes in v2:
time: 152 us
  Pallas kernels  146 us (96%)
  local copies, waits for them, and re-layouts  5 us (3%)
    pallas_call x1, Pallas kernels, exchange(): pl.pallas_call(functools.partial(kernel, n, shifts), out_shape=(pltpu.VME...  146 us
    unnamed x3, local copies, waits for them, and re-layouts  5 us

profile of v2, /device:TPU:18, one launch (start us, length us, event | category | flops | bytes accessed | tf_op | source)
XLA Modules:
  0.0 152.1 jit_solution(14540459985737527074)
XLA Ops:
  0.6 146.5 %shard_map.94 = (bf16[512,1024]{1,0:T(8,128)(2,1)S(1)}, f32[512,2048]{1,0:T(8,128)S(1)}, f32[1024,1024]{1,0:T(8,128)S(1)}) custom-call(s32[1,512]{1,0:T(1,128)} %bitcast.12, f32[1,512]{1,0:T(1,128)} %bitcast.13, bf16[512,1024]{1,0:T(8,128)(2,1)} %tokens.1, bf16[512,1024]{1,0:T(8,128)(2,1)} %cotangent.1, s32[32,2048]{1,0:T(8,128)} %bitcast.11, ...), custom_call_target="tpu_custom_call" | custom-call | flops 21474836480 | bytes 41943040 | tf_op jit(solution)/shard_map/pallas_call | solution.py:361
  147.1 1.0 copy.13
  148.1 2.0 %copy.14 = f32[1,512,2048]{2,1,0:T(8,128)} copy(f32[1,512,2048]{2,1,0:T(8,128)S(1)} %bitcast.8) | data formatting | bytes 8388608
  150.1 2.0 %copy.15 = f32[1,1024,1024]{2,1,0:T(8,128)} copy(f32[1,1024,1024]{2,1,0:T(8,128)S(1)} %bitcast.7) | data formatting | bytes 8388608

commit v3 on v2

--- a/solution.py
+++ b/solution.py
@@ -36,8 +36,8 @@
 def kernel(
     n, shifts,
     ids_in, prob_in, tokens, cotangent, keep, w_in, w_out,
-    mixed, grad_in, grad_out,
-    ids, prob, own_x, own_g, keep_raw, keep_rows, slot, columns_of,
+    grad_in, grad_out, total, chosen_last, last_rows, columns_of,
+    ids, prob, own_x, own_g, keep_raw, keep_rows, slot,
     sent, sent_grad, back,
     weight_in, weight_out, rows_x, rows_g, rows_o, hidden, factor, dpre,
     give_out, give_in, came_out, came_in,
@@ -55,7 +55,6 @@
     tile = tile_of(ff, 512)
     wide = tile_of(width, 256)
     count = own_x.shape[0]
-    total = factor.at[pl.ds(0, count), pl.ds(0, width)]
 
     def load(i):
         source, target = (
@@ -305,6 +304,10 @@
             found = (lax.rem(plane + shift, shifts) * group + turn) * cap + lax.rem(inside, cap)
             place = jnp.where((inside >= 0) & (inside < many), found, place)
         chosen = jnp.where(place == columns_of[:, 0:1].astype(jnp.int32), 1.0, 0.0).astype(jnp.bfloat16)
+        if last:
+            chosen_last[...] = chosen
+            if first:
+                total[...] = jnp.zeros_like(total)
         for shift, low_turn, turns in pieces:
             def arrived(turn):
                 @pl.when(shift * group + turn > 0)
@@ -312,6 +315,11 @@
                     o_copy(shift, turn).wait_recv()
 
             each(low_turn, low_turn + turns, arrived)
+        if last:
+            for at, (shift, low_turn, turns) in enumerate(pieces):
+                last_rows[pl.ds(at * many, many), :] = back[
+                    pl.ds(shift * group + low_turn, turns)].reshape(many, width)
+            return
         for j in range(width // wide):
             columns = pl.ds(j * wide, wide)
             block = jnp.concatenate([
@@ -321,10 +329,7 @@
             added = jnp.dot(chosen, block, preferred_element_type=jnp.float32)
             if not first:
                 added += total[:, columns]
-            if last:
-                mixed[:, columns] = (columns_of[:, 1:2] * added).astype(jnp.bfloat16)
-            else:
-                total[:, columns] = added
+            total[:, columns] = added
 
     far = [near_first(i, -1) for i in range(2, shifts)]
     half, quarter = group // 2, group // 4
@@ -353,6 +358,7 @@
     count, width = tokens.shape
     ff = w_in.shape[1]
     shifts = 4 if n % 4 == 0 else 1
+    last = n // 8 * cap if n % 16 == 0 else n // shifts * cap
     dma = pltpu.SemaphoreType.DMA
     f32, bf16 = jnp.float32, jnp.bfloat16
     whole = pl.BlockSpec(memory_space=pl.ANY)
@@ -361,12 +367,15 @@
     return pl.pallas_call(
         functools.partial(kernel, n, shifts),
         out_shape=(
-            pltpu.VMEM((count, width), bf16),
             pltpu.VMEM((width // 2, ff), f32),
             pltpu.VMEM((ff // 2, width), f32),
+            pltpu.VMEM((count, width), f32),
+            pltpu.VMEM((count, last), bf16),
+            pltpu.VMEM((last, width), bf16),
+            pltpu.VMEM((count, 128), f32),
         ),
         in_specs=[whole] * 7,
-        out_specs=(near, near, near),
+        out_specs=(near,) * 6,
         scratch_shapes=[
             pltpu.VMEM((1, count), jnp.int32),
             pltpu.VMEM((1, count), f32),
@@ -375,7 +384,6 @@
             pltpu.VMEM(keep.shape, jnp.int32),
             pltpu.VMEM((n, 1, ff), f32),
             pltpu.VMEM((1, count), jnp.int32),
-            pltpu.VMEM((count, 128), f32),
             pltpu.VMEM((n, cap, width), bf16),
             pltpu.VMEM((n, cap, width), bf16),
             pltpu.VMEM((n, cap, width), bf16),
@@ -396,18 +404,60 @@
         ],
         cost_estimate=pl.CostEstimate(flops=flops, bytes_accessed=40 << 20, transcendentals=n * cap * ff),
         compiler_params=pltpu.CompilerParams(
-            collective_id=0, has_side_effects=True, vmem_limit_bytes=52 << 20
+            collective_id=0, has_side_effects=True, vmem_limit_bytes=50 << 20
         ),
     )(ids, prob, tokens, cotangent, keep, w_in, w_out)
+
+
+def closing(
+    sum_in, sum_out, total, chosen, rows, columns_of, mixed, grad_in, grad_out, held, sem
+):
+    copies = [
+        pltpu.make_async_copy(source, target, sem.at[i])
+        for i, (source, target) in enumerate(((sum_in, grad_in), (sum_out, grad_out), (held, mixed)))
+    ]
+    copies[0].start()
+    copies[1].start()
+    width = held.shape[1]
+    wide = tile_of(width, 256)
+    for j in range(width // wide):
+        columns = pl.ds(j * wide, wide)
+        added = total[:, columns] + jnp.dot(
+            chosen[...], rows[:, columns], preferred_element_type=jnp.float32)
+        held[:, columns] = (columns_of[:, 1:2] * added).astype(jnp.bfloat16)
+    copies[2].start()
+    for copy in copies:
+        copy.wait()
+
+
+def close(sum_in, sum_out, total, chosen, rows, columns_of):
+    near = pl.BlockSpec(memory_space=pltpu.VMEM)
+    whole = pl.BlockSpec(memory_space=pl.ANY)
+    count, width = total.shape
+    args = (sum_in, sum_out, total, chosen, rows, columns_of)
+    return pl.pallas_call(
+        closing,
+        out_shape=(
+            jax.ShapeDtypeStruct((count, width), jnp.bfloat16),
+            jax.ShapeDtypeStruct(sum_in.shape, sum_in.dtype),
+            jax.ShapeDtypeStruct(sum_out.shape, sum_out.dtype),
+        ),
+        in_specs=[near] * 6,
+        out_specs=(whole, whole, whole),
+        scratch_shapes=[pltpu.VMEM((count, width), jnp.bfloat16), pltpu.SemaphoreType.DMA((3,))],
+        cost_estimate=pl.CostEstimate(
+            flops=2 * chosen.size * width, bytes_accessed=9 << 20, transcendentals=0),
+        compiler_params=pltpu.CompilerParams(vmem_limit_bytes=8 << 20),
+    )(*[pltpu.with_memory_space_constraint(arg, pltpu.VMEM) for arg in args])
 
 
 def shards(tokens, expert_id, router_prob, keep_mask, w_in, w_out, cotangent):
     count = tokens.shape[0]
     n = lax.axis_size("expert")
-    mixed, grad_in, grad_out = exchange(
+    mixed, grad_in, grad_out = close(*exchange(
         n, 2 * count // n, expert_id.reshape(1, count), router_prob.reshape(1, count),
         tokens, cotangent, keep_mask[0], w_in[0], w_out[0],
-    )
+    ))
     return (mixed, grad_in[None], grad_out[None])
 
 

time: 152 us -> 151 us (level)
  local copies, waits for them, and re-layouts: 5 us -> 0 us
  Pallas kernels: 146 us -> 150 us
    unnamed x3 -> x0, local copies, waits for them, and re-layouts: 5 us -> none
    pallas_call x0 -> x1, Pallas kernels: none -> 3.64 us  [close(): pl.pallas_call(closing, out_shape=(jax.ShapeDtypeStruct((count, width), j...]
where the time goes in v3:
time: 151 us; the launch traced here: 150 us
  Pallas kernels  150 us (99%)
    pallas_call x1, Pallas kernels, exchange(): pl.pallas_call(functools.partial(kernel, n, shifts), out_shape=(pltpu.VME...  146 us
    pallas_call x1, Pallas kernels, close(): pl.pallas_call(closing, out_shape=(jax.ShapeDtypeStruct((count, width), j...  3.64 us

profile of v3, /device:TPU:18, one launch (start us, length us, event | category | flops | bytes accessed | tf_op | source)
XLA Modules:
  0.0 150.4 jit_solution(14206721204040130785)
XLA Ops:
  0.6 146.2 %shard_map.94 = (f32[512,2048]{1,0:T(8,128)S(1)}, f32[1024,1024]{1,0:T(8,128)S(1)}, f32[512,1024]{1,0:T(8,128)S(1)}, bf16[512,128]{1,0:T(8,128)(2,1)S(1)}, bf16[...) custom-call(s32[1,512]{1,0:T(1,128)} %bitcast.12, f32[1,512]{1,0:T(1,128)} %bitcast.13, bf16[512,1024]{1,0:T(8,128)(2,1)} %tokens.1, ...), custom_call_target="tpu_custom_call" | custom-call | flops 21474836480 | bytes 41943040 | tf_op jit(solution)/shard_map/pallas_call | solution.py:367
  146.8 3.6 %shard_map.95 = (bf16[512,1024]{1,0:T(8,128)(2,1)}, f32[512,2048]{1,0:T(8,128)}, f32[1024,1024]{1,0:T(8,128)}) custom-call(f32[512,2048]{1,0:T(8,128)S(1)} %get-tuple-element.12.sum_in, f32[1024,1024]{1,0:T(8,128)S(1)} %get-tuple-element.13.sum_out, f32[512,1024]{1,0:T(8,128)S(1)} %get-tuple-element.14.total, bf16[512,128]{1,0:T(8,128)(2,1)S(1)} %get-tuple-element.15.chosen, ...), custom_call_target="tpu_custom_call" | custom-call | flops 134217728 | bytes 9437184 | tf_op jit(solution)/shard_map/pallas_call | solution.py:438

commit v4 on v3

--- a/solution.py
+++ b/solution.py
@@ -170,6 +170,16 @@
     load(0).wait()
     for i in range(1, 5):
         load(i).start()
+    def turned(shift, step):
+        def one(i):
+            turn = lax.rem(i + core * (group // 2), group)
+
+            @pl.when(shift * group + turn > 0)
+            def _():
+                step(shift, turn)
+
+        each(0, group, one)
+
     def send_x(i):
         dispatch(own_x, sent, send_order(i))
 
@@ -177,7 +187,7 @@
         def _():
             pl.semaphore_wait(barrier, n)
 
-        blocks(send_order(i), start(x_copy))
+        turned(send_order(i), start(x_copy))
 
     each(0, shifts, send_x)
     own_copy(0).start()
@@ -186,7 +196,7 @@
 
     def send_g(i):
         dispatch(own_g, sent_grad, send_order(i))
-        blocks(send_order(i), start(g_copy))
+        turned(send_order(i), start(g_copy))
 
     each(0, shifts, send_g)
     own_copy(1).start()
@@ -238,7 +248,7 @@
             own_copy(2).start()
 
     each(0, shifts, forward)
-    each(0, shifts - shifts // 2, lambda i: blocks(near_first(shifts - 1 - i, 1), start(o_copy)))
+    each(0, shifts - shifts // 2, lambda i: turned(near_first(shifts - 1 - i, 1), start(o_copy)))
 
     def backward(i):
         shift = near_first(i, 1)
@@ -336,9 +346,11 @@
     if shifts == 4 and quarter * 4 == group:
         merge([(0, 0, group)], True, False)
         merge([(near_first(1, -1), 0, group)], False, False)
-        merge([(shift, 0, half) for shift in far], False, False)
-        merge([(shift, half, quarter) for shift in far], False, False)
-        final = [(shift, half + quarter, quarter) for shift in far]
+        begin = core * half
+        merge([(shift, begin, half) for shift in far], False, False)
+        begin = lax.rem(begin + half, group)
+        merge([(shift, begin, quarter) for shift in far], False, False)
+        final = [(shift, begin + quarter, quarter) for shift in far]
     else:
         for shift in range(shifts - 1):
             merge([(shift, 0, group)], shift == 0, False)

time: 151 us -> 150 us (level); the launches traced: 150 us -> 147 us
  Pallas kernels: 150 us -> 146 us
    pallas_call x1, Pallas kernels: 146 us -> 142 us  [exchange(): pl.pallas_call(functools.partial(kernel, n, shifts), out_shape=(pltpu.VME...]
where the time goes in v4:
time: 150 us; the launch traced here: 147 us
  Pallas kernels  146 us (97%)
    pallas_call x1, Pallas kernels, exchange(): pl.pallas_call(functools.partial(kernel, n, shifts), out_shape=(pltpu.VME...  142 us
    pallas_call x1, Pallas kernels, close(): pl.pallas_call(closing, out_shape=(jax.ShapeDtypeStruct((count, width), j...  3.64 us

profile of v4, /device:TPU:18, one launch (start us, length us, event | category | flops | bytes accessed | tf_op | source)
XLA Modules:
  0.0 146.7 jit_solution(8781639752743619902)
XLA Ops:
  0.6 142.4 %shard_map.94 = (f32[512,2048]{1,0:T(8,128)S(1)}, f32[1024,1024]{1,0:T(8,128)S(1)}, f32[512,1024]{1,0:T(8,128)S(1)}, bf16[512,128]{1,0:T(8,128)(2,1)S(1)}, bf16[...) custom-call(s32[1,512]{1,0:T(1,128)} %bitcast.12, f32[1,512]{1,0:T(1,128)} %bitcast.13, bf16[512,1024]{1,0:T(8,128)(2,1)} %tokens.1, ...), custom_call_target="tpu_custom_call" | custom-call | flops 21474836480 | bytes 41943040 | tf_op jit(solution)/shard_map/pallas_call | solution.py:379
  143.1 3.6 %shard_map.95 = (bf16[512,1024]{1,0:T(8,128)(2,1)}, f32[512,2048]{1,0:T(8,128)}, f32[1024,1024]{1,0:T(8,128)}) custom-call(f32[512,2048]{1,0:T(8,128)S(1)} %get-tuple-element.12.sum_in, f32[1024,1024]{1,0:T(8,128)S(1)} %get-tuple-element.13.sum_out, f32[512,1024]{1,0:T(8,128)S(1)} %get-tuple-element.14.total, bf16[512,128]{1,0:T(8,128)(2,1)S(1)} %get-tuple-element.15.chosen, ...), custom_call_target="tpu_custom_call" | custom-call | flops 134217728 | bytes 9437184 | tf_op jit(solution)/shard_map/pallas_call | solution.py:450
